TPU v7x, 32 devices: a whole 2x2x4 slice. The times are simulated.
32 devices in a mesh: grp: 4 (over y, x), section: 2 (over core), row: 4 (over z).
Axes of the slice: x: 2, y: 2, z: 4, core: 2. Of those that a mesh axis runs over, the one named last changes fastest.
Arguments:
- matrices: float32 [4, 8192, 8192], P('grp', 'row', 'section'), parts along dimension 0, may hold values from -57 to 57, as said below
Outputs:
- reduced: float32 [4, 8192, 8192], P('grp', 'row', 'section'), parts along dimension 0
There are 4 independent parts, one for each index of `grp`. A program takes and returns all parts, laid end to end along the dimension named above; each array names one. Nothing has to cross between parts.
Inputs may be any that keep to these rules, and one draw needn't show every extreme that they name: `matrices`: each matrix is exactly symmetric.
All inputs are finite; a program needn't handle non-finite values.
Results may differ from a plain program's by a relative error of at most 0.00023.
Values sent between devices are 32-bit elements; how exact they have to be, the bound alone decides.
No kernel may reach another device: no remote copies, remote signals or barrier semaphores. Data moves between devices by JAX's collectives and lax.ppermute only.
A program may use at most 128 MiB of HBM per device.

v0:
```python
import jax
import jax.numpy as jnp
from jax import lax
from jax.sharding import PartitionSpec as P

NB = 8
highest = lax.Precision.HIGHEST


def broadcast(value, axis, source):
    kept = jnp.where(lax.axis_index(axis) == source, value, 0).astype(value.dtype)
    return lax.psum(kept, axis)


def local(matrices):
    height = matrices.shape[1]
    breadth = matrices.shape[2]
    order = height * lax.axis_size("row")
    row_start = lax.axis_index("row") * height
    col_start = lax.axis_index("section") * breadth
    owned = jnp.swapaxes(matrices[:, :, :NB], 1, 2)
    owned = broadcast(owned, "section", 0)
    panel_cols = lax.all_gather(owned, "row", axis=2, tiled=True)
    positions = jnp.arange(order, dtype=jnp.int32)
    left_list = []
    right_list = []
    for column in range(NB):
        current = panel_cols[:, column, :]
        if column > 0:
            lefts = jnp.stack(left_list, 1)
            rights = jnp.stack(right_list, 1)
            current = current - jnp.einsum(
                "mkn,mk->mn", lefts, rights[:, :, column], precision=highest
            )
            current = current - jnp.einsum(
                "mkn,mk->mn", rights, lefts[:, :, column], precision=highest
            )
        below = jnp.where(positions[None, :] > column, current, 0.0)
        length = jnp.sqrt(jnp.sum(below * below, axis=1))
        reflector = below + jnp.where(positions[None, :] == column + 1, length[:, None], 0.0)
        scaling = 2.0 / (jnp.sum(reflector * reflector, axis=1) + 1e-06)
        row_part = lax.dynamic_slice_in_dim(reflector, row_start, height, 1)
        partial_cols = jnp.einsum("mij,mi->mj", matrices, row_part, precision=highest)
        summed_cols = lax.psum(partial_cols, "row")
        image = lax.all_gather(summed_cols, "section", axis=1, tiled=True)
        if column > 0:
            right_dots = jnp.einsum("mkn,mn->mk", rights, reflector, precision=highest)
            left_dots = jnp.einsum("mkn,mn->mk", lefts, reflector, precision=highest)
            image = image - jnp.einsum("mkn,mk->mn", lefts, right_dots, precision=highest)
            image = image - jnp.einsum("mkn,mk->mn", rights, left_dots, precision=highest)
        corrected = scaling[:, None] * image
        inner = jnp.sum(corrected * reflector, axis=1)
        partner = corrected - (0.5 * scaling * inner)[:, None] * reflector
        left_list.append(reflector)
        right_list.append(partner)
    lefts = jnp.stack(left_list, 1)
    rights = jnp.stack(right_list, 1)
    rows_left = lax.dynamic_slice_in_dim(lefts, row_start, height, 2)
    rows_right = lax.dynamic_slice_in_dim(rights, row_start, height, 2)
    cols_left = lax.dynamic_slice_in_dim(lefts, col_start, breadth, 2)
    cols_right = lax.dynamic_slice_in_dim(rights, col_start, breadth, 2)
    reduced = matrices - jnp.einsum("mki,mkj->mij", rows_left, cols_right, precision=highest)
    reduced = reduced - jnp.einsum("mki,mkj->mij", rows_right, cols_left, precision=highest)
    return reduced


def solution(mesh):
    in_specs = (P("grp", "row", "section"),)
    out_specs = P("grp", "row", "section")
    return jax.shard_map(local, mesh=mesh, in_specs=in_specs, out_specs=out_specs, check_vma=False)
```

profile of v0, /device:TPU:0, one launch (start us, length us, event | category | flops | bytes accessed | tf_op | source)
XLA Modules:
  0.0 484.6 jit_solution(7150372267628386064)
XLA Ops:
  6.5 1.3 slice.69
  8.1 0.6 select_bitcast_fusion
  8.8 21.3 %all-reduce.2.cloned.1.call-done = f32[1,8,2048]{2,1,0:T(8,128)} async-done(((f32[1,8,2048]{2,1,0:T(8,128)}), f32[1,8,2048]{2,1,0:T(8,128)}) %all-reduce.2.cloned.1.call-update) | async-done | bytes 65552 | tf_op jit(solution)/shard_map/psum | solution.py:12
  30.1 14.4 %all_gather.27 = f32[1,8,8192]{2,1,0:T(8,128)S(1)} all-gather(f32[1,8,2048]{2,1,0:T(8,128)} %all-reduce.2.cloned.1.call-done), channel_id=1, replica_groups=mesh['grp'=4,'section'=2,'row'=4] {'row'}, dimensions={2}, use_global_device_ids=true | all-gather | bytes 327680 | tf_op jit(solution)/shard_map/all_gather | solution.py:23
  44.5 0.7 multiply_reduce_fusion.25
  45.9 0.7 multiply_reduce_fusion.24
  46.8 0.7 slice.95
  47.4 19.5 %fusion.14 = f32[1,4096]{1,0:T(1,128)S(1)} fusion(f32[1,2048,4096]{2,1,0:T(8,128)} %param.1, f32[1,8192]{1,0:T(1,128)S(1)} %get-tuple-element.26, s32[]{:T(128)S(6)} %select_n.146), kind=kOutput, calls=%fused_computation.16 | convolution fusion | flops 100663296 | bytes 33579012 | tf_op jit(solution)/shard_map/mij,mi->mj/dot_general | solution.py:43
  66.9 19.3 %psum.64 = f32[1,4096]{1,0:T(1,128)S(1)} all-reduce(f32[1,4096]{1,0:T(1,128)S(1)} %fusion.14), channel_id=1, replica_groups=mesh['grp'=4,'section'=2,'row'=4] {'row'}, use_global_device_ids=true, to_apply=%region_3.4 | all-reduce | flops 4096 | bytes 32768 | tf_op jit(solution)/shard_map/psum | solution.py:44
  86.2 1.8 all_gather.28
  88.7 0.7 multiply_reduce_fusion.23
  90.6 1.9 multiply_reduce_fusion.22
  93.2 0.7 multiply_reduce_fusion.21
  94.8 19.5 %fusion.12 = f32[1,4096]{1,0:T(1,128)S(1)} fusion(f32[2048,1]{0,1:T(1,128)S(1)} %bitcast.471, f32[1,2048,4096]{2,1,0:T(8,128)} %param.1), kind=kOutput, calls=%fused_computation.14 | convolution fusion | flops 100663296 | bytes 33579008 | tf_op jit(solution)/shard_map/mij,mi->mj/dot_general | solution.py:43
  114.3 15.5 %psum.65 = f32[1,4096]{1,0:T(1,128)S(1)} all-reduce(f32[1,4096]{1,0:T(1,128)S(1)} %fusion.12), channel_id=1, replica_groups=mesh['grp'=4,'section'=2,'row'=4] {'row'}, use_global_device_ids=true, to_apply=%region_7.8 | all-reduce | flops 4096 | bytes 32768 | tf_op jit(solution)/shard_map/psum | solution.py:44
  129.8 2.1 all_gather.29
  131.9 1.3 broadcast_multiply_fusion.7
  133.2 0.7 multiply_reduce_fusion.20
  135.6 0.6 multiply_reduce_fusion.19
  136.9 0.6 multiply_reduce_fusion.18
  137.5 0.7 convolution_bitcast_fusion.10
  138.1 0.7 convolution_bitcast_fusion.11
  139.5 19.5 %fusion.10 = f32[1,4096]{1,0:T(1,128)S(1)} fusion(f32[2048,1]{0,1:T(1,128)S(1)} %bitcast.466, f32[1,2048,4096]{2,1,0:T(8,128)} %param.1), kind=kOutput, calls=%fused_computation.12 | convolution fusion | flops 100663296 | bytes 33579008 | tf_op jit(solution)/shard_map/mij,mi->mj/dot_general | solution.py:43
  159.1 16.3 %psum.66 = f32[1,4096]{1,0:T(1,128)S(1)} all-reduce(f32[1,4096]{1,0:T(1,128)S(1)} %fusion.10), channel_id=1, replica_groups=mesh['grp'=4,'section'=2,'row'=4] {'row'}, use_global_device_ids=true, to_apply=%region_11.12 | all-reduce | flops 4096 | bytes 32768 | tf_op jit(solution)/shard_map/psum | solution.py:44
  175.3 2.3 all_gather.30
  178.1 1.0 multiply_reduce_fusion.17
  182.6 0.6 multiply_reduce_fusion.15
  183.2 0.7 convolution_bitcast_fusion.8
  183.9 0.7 convolution_bitcast_fusion.9
  185.3 19.5 %fusion.8 = f32[1,4096]{1,0:T(1,128)S(1)} fusion(f32[2048,1]{0,1:T(1,128)S(1)} %bitcast.467, f32[1,2048,4096]{2,1,0:T(8,128)} %param.1), kind=kOutput, calls=%fused_computation.10 | convolution fusion | flops 100663296 | bytes 33579008 | tf_op jit(solution)/shard_map/mij,mi->mj/dot_general | solution.py:43
  204.8 15.6 %psum.67 = f32[1,4096]{1,0:T(1,128)S(1)} all-reduce(f32[1,4096]{1,0:T(1,128)S(1)} %fusion.8), channel_id=1, replica_groups=mesh['grp'=4,'section'=2,'row'=4] {'row'}, use_global_device_ids=true, to_apply=%region_15.16 | all-reduce | flops 4096 | bytes 32768 | tf_op jit(solution)/shard_map/psum | solution.py:44
  220.3 2.0 all_gather.31
  222.8 1.1 multiply_reduce_fusion.14
  227.2 0.6 multiply_reduce_fusion.12
  227.8 0.7 convolution_bitcast_fusion.6
  228.5 0.7 convolution_bitcast_fusion.7
  229.9 19.5 %fusion.6 = f32[1,4096]{1,0:T(1,128)S(1)} fusion(f32[2048,1]{0,1:T(1,128)S(1)} %bitcast.468, f32[1,2048,4096]{2,1,0:T(8,128)} %param.1), kind=kOutput, calls=%fused_computation.8 | convolution fusion | flops 100663296 | bytes 33579008 | tf_op jit(solution)/shard_map/mij,mi->mj/dot_general | solution.py:43
  249.4 16.3 %psum.68 = f32[1,4096]{1,0:T(1,128)S(1)} all-reduce(f32[1,4096]{1,0:T(1,128)S(1)} %fusion.6), channel_id=1, replica_groups=mesh['grp'=4,'section'=2,'row'=4] {'row'}, use_global_device_ids=true, to_apply=%region_19.20 | all-reduce | flops 4096 | bytes 32768 | tf_op jit(solution)/shard_map/psum | solution.py:44
  265.7 2.0 all_gather.32
  268.0 1.0 multiply_reduce_fusion.11
  272.6 0.6 multiply_reduce_fusion.9
  273.2 0.7 convolution_bitcast_fusion.4
  273.9 0.7 convolution_bitcast_fusion.5
  275.3 19.5 %fusion.4 = f32[1,4096]{1,0:T(1,128)S(1)} fusion(f32[2048,1]{0,1:T(1,128)S(1)} %bitcast.469, f32[1,2048,4096]{2,1,0:T(8,128)} %param.1), kind=kOutput, calls=%fused_computation.6 | convolution fusion | flops 100663296 | bytes 33579008 | tf_op jit(solution)/shard_map/mij,mi->mj/dot_general | solution.py:43
  294.8 15.6 %psum.69 = f32[1,4096]{1,0:T(1,128)S(1)} all-reduce(f32[1,4096]{1,0:T(1,128)S(1)} %fusion.4), channel_id=1, replica_groups=mesh['grp'=4,'section'=2,'row'=4] {'row'}, use_global_device_ids=true, to_apply=%region_23.24 | all-reduce | flops 4096 | bytes 32768 | tf_op jit(solution)/shard_map/psum | solution.py:44
  310.4 2.1 all_gather.33
  312.8 1.0 multiply_reduce_fusion.8
  317.5 0.6 multiply_reduce_fusion.6
  318.1 0.7 convolution_bitcast_fusion.2
  318.8 0.7 convolution_bitcast_fusion.3
  320.2 19.5 %fusion.2 = f32[1,4096]{1,0:T(1,128)S(1)} fusion(f32[2048,1]{0,1:T(1,128)S(1)} %bitcast.470, f32[1,2048,4096]{2,1,0:T(8,128)} %param.1), kind=kOutput, calls=%fused_computation.4 | convolution fusion | flops 100663296 | bytes 33579008 | tf_op jit(solution)/shard_map/mij,mi->mj/dot_general | solution.py:43
  339.7 16.2 %psum.70 = f32[1,4096]{1,0:T(1,128)S(1)} all-reduce(f32[1,4096]{1,0:T(1,128)S(1)} %fusion.2), channel_id=1, replica_groups=mesh['grp'=4,'section'=2,'row'=4] {'row'}, use_global_device_ids=true, to_apply=%region_27.28 | all-reduce | flops 4096 | bytes 32768 | tf_op jit(solution)/shard_map/psum | solution.py:44
  355.9 2.3 all_gather.34
  358.5 1.0 multiply_reduce_fusion.5
  362.0 0.6 multiply_reduce_fusion.4
  363.3 0.6 multiply_reduce_fusion.3
  363.9 0.7 convolution_bitcast_fusion
  364.6 0.7 convolution_bitcast_fusion.1
  366.0 19.5 %fusion = f32[1,4096]{1,0:T(1,128)S(1)} fusion(f32[2048,1]{0,1:T(1,128)S(1)} %bitcast.465, f32[1,2048,4096]{2,1,0:T(8,128)} %param.1), kind=kOutput, calls=%fused_computation.2 | convolution fusion | flops 100663296 | bytes 33579008 | tf_op jit(solution)/shard_map/mij,mi->mj/dot_general | solution.py:43
  385.5 15.6 %psum.71 = f32[1,4096]{1,0:T(1,128)S(1)} all-reduce(f32[1,4096]{1,0:T(1,128)S(1)} %fusion), channel_id=1, replica_groups=mesh['grp'=4,'section'=2,'row'=4] {'row'}, use_global_device_ids=true, to_apply=%region_31.32 | all-reduce | flops 4096 | bytes 32768 | tf_op jit(solution)/shard_map/psum | solution.py:44
  401.1 2.0 all_gather.35
  403.4 1.0 multiply_reduce_fusion.2
  405.9 30.3 %fusion.47 = f32[2048,4096]{1,0:T(8,128)} fusion(f32[1,8,8192]{2,1,0:T(8,128)S(1)} %stack.172, s32[]{:T(128)S(6)} %select_n.161, f32[1,8,8192]{2,1,0:T(8,128)S(1)} %stack.84, s32[]{:T(128)S(6)} %select_n.146), kind=kOutput, calls=%fused_computation.77 | convolution fusion | flops 805306368 | bytes 33751048 | tf_op jit(solution)/shard_map/mki,mkj->mij/dot_general | solution.py:62
  436.3 41.3 %bitcast_subtract_fusion = f32[1,2048,4096]{2,1,0:T(8,128)} fusion(f32[1,2048,4096]{2,1,0:T(8,128)} %param.1, f32[2048,4096]{1,0:T(8,128)} %fusion.47, f32[1,8,8192]{2,1,0:T(8,128)S(1)} %stack.84, s32[]{:T(128)S(6)} %select_n.161, f32[1,8,8192]{2,1,0:T(8,128)S(1)} %stack.172, s32[]{:T(128)S(6)} %select_n.146), kind=kOutput, calls=%fused_computation | convolution fusion | flops 822083584 | bytes 100859912 | tf_op jit(solution)/shard_map/mki,mkj->mij/dot_general | solution.py:63
  (73 shorter events, 15.7 us)
Async XLA Ops:
  6.5 23.6 %all-reduce.2.cloned.1.call-start = ((), (), s32[]{:S(2)}) async-start(), calls=%async_computation | async-start | bytes 131072 | tf_op jit(solution)/shard_map/psum | solution.py:12
Sparse Core Ops, SparseCore 0:
  9.6 20.4 all-reduce.1
where the time goes:
time: 492 us; the launch traced here: 485 us
  matrix products  249 us (51%)
  blocking collectives  161 us (33%)
  between operations  30.3 us (6%)
  waiting for transfers between devices  21.3 us (4%)
  other arithmetic  15.9 us (3%)
  local copies, waits for them, and re-layouts  7.2 us (1%)
    dot_general x8, matrix products, local(): jnp.einsum('mij,mi->mj', matrices, row_part, precision=highest)  156 us
    psum x8, blocking collectives, local(): summed_cols = lax.psum(partial_cols, 'row')  130 us
    dot_general x1, matrix products, local(): jnp.einsum('mki,mkj->mij', rows_right, cols_left, precision=highest)  41.3 us
    dot_general x1, matrix products, local(): jnp.einsum('mki,mkj->mij', rows_left, cols_right, precision=highest)  30.3 us
    psum x1, waiting for transfers between devices, broadcast(): return lax.psum(kept, axis)  21.3 us
    all_gather x8, blocking collectives, local(): image = lax.all_gather(summed_cols, 'section', axis=1, tiled=True)  16.6 us
    all_gather x1, blocking collectives, local(): panel_cols = lax.all_gather(owned, 'row', axis=2, tiled=True)  14.4 us
  transfers between devices with their start and end apart: 1, of which 1 were waited for; matrix products, arithmetic and copies ran while one was open for 0% of the time, Pallas kernels for 0%

commit v1 on v0

--- a/solution.py
+++ b/solution.py
@@ -41,7 +41,7 @@
         scaling = 2.0 / (jnp.sum(reflector * reflector, axis=1) + 1e-06)
         row_part = lax.dynamic_slice_in_dim(reflector, row_start, height, 1)
         partial_cols = jnp.einsum("mij,mi->mj", matrices, row_part, precision=highest)
-        summed_cols = lax.psum(partial_cols, "row")
+        summed_cols = jnp.sum(lax.all_gather(partial_cols, "row"), axis=0)
         image = lax.all_gather(summed_cols, "section", axis=1, tiled=True)
         if column > 0:
             right_dots = jnp.einsum("mkn,mn->mk", rights, reflector, precision=highest)

time: 492 us -> 467 us (0.949)
  blocking collectives: 161 us -> 136 us
    psum x8 -> x0, blocking collectives: 130 us -> none  [local(): summed_cols = lax.psum(partial_cols, 'row')]
    all_gather x0 -> x8, blocking collectives: none -> 105 us  [local(): summed_cols = jnp.sum(lax.all_gather(partial_cols, 'row'), axis=0)]
where the time goes in v1:
time: 467 us; the launch traced here: 460 us
  matrix products  245 us (52%)
  blocking collectives  136 us (29%)
  between operations  30.6 us (7%)
  waiting for transfers between devices  21.3 us (5%)
  other arithmetic  19.6 us (4%)
  local copies, waits for them, and re-layouts  7.41 us (2%)
    dot_general x8, matrix products, local(): jnp.einsum('mij,mi->mj', matrices, row_part, precision=highest)  156 us
    all_gather x8, blocking collectives, local(): summed_cols = jnp.sum(lax.all_gather(partial_cols, 'row'), axis=0)  105 us
    dot_general x1, matrix products, local(): jnp.einsum('mki,mkj->mij', rows_right, cols_left, precision=highest)  41.4 us
    dot_general x1, matrix products, local(): jnp.einsum('mki,mkj->mij', rows_left, cols_right, precision=highest)  30.3 us
    psum x1, waiting for transfers between devices, broadcast(): return lax.psum(kept, axis)  21.3 us
    all_gather x8, blocking collectives, local(): image = lax.all_gather(summed_cols, 'section', axis=1, tiled=True)  16.5 us
    all_gather x1, blocking collectives, local(): panel_cols = lax.all_gather(owned, 'row', axis=2, tiled=True)  14.4 us
  transfers between devices with their start and end apart: 1, of which 1 were waited for; matrix products, arithmetic and copies ran while one was open for 0% of the time, Pallas kernels for 0%

profile of v1, /device:TPU:0, one launch (start us, length us, event | category | flops | bytes accessed | tf_op | source)
XLA Modules:
  0.0 460.1 jit_solution(17159064692361487187)
XLA Ops:
  6.5 1.3 slice.69
  8.1 0.6 select_bitcast_fusion
  8.8 21.3 %all-reduce.2.cloned.1.call-done = f32[1,8,2048]{2,1,0:T(8,128)} async-done(((f32[1,8,2048]{2,1,0:T(8,128)}), f32[1,8,2048]{2,1,0:T(8,128)}) %all-reduce.2.cloned.1.call-update) | async-done | bytes 65552 | tf_op jit(solution)/shard_map/psum | solution.py:12
  30.1 14.4 %all_gather.75 = f32[1,8,8192]{2,1,0:T(8,128)S(1)} all-gather(f32[1,8,2048]{2,1,0:T(8,128)} %all-reduce.2.cloned.1.call-done), channel_id=1, replica_groups=mesh['grp'=4,'section'=2,'row'=4] {'row'}, dimensions={2}, use_global_device_ids=true | all-gather | bytes 327680 | tf_op jit(solution)/shard_map/all_gather | solution.py:23
  44.5 0.7 multiply_reduce_fusion.25
  45.9 0.7 multiply_reduce_fusion.24
  46.8 0.7 slice.95
  47.4 19.5 %fusion.14 = f32[1,4096]{1,0:T(1,128)S(1)} fusion(f32[1,2048,4096]{2,1,0:T(8,128)} %param.1, f32[1,8192]{1,0:T(1,128)S(1)} %get-tuple-element.38, s32[]{:T(128)S(6)} %select_n.146), kind=kOutput, calls=%fused_computation.16 | convolution fusion | flops 100663296 | bytes 33579012 | tf_op jit(solution)/shard_map/mij,mi->mj/dot_general | solution.py:43
  66.9 13.2 %all-gather = f32[16384]{0:T(1024)S(1)} all-gather(f32[4096]{0:T(1024)S(1)} %bitcast.469), channel_id=2, replica_groups=mesh['grp'=4,'section'=2,'row'=4] {'row'}, dimensions={0}, use_global_device_ids=true | all-gather | bytes 81920 | tf_op jit(solution)/shard_map/all_gather | solution.py:44
  80.2 1.8 all-gather.1
  82.7 0.7 multiply_reduce_fusion.23
  84.7 1.9 multiply_reduce_fusion.22
  87.2 0.7 multiply_reduce_fusion.1
  88.7 19.5 %fusion.12 = f32[1,4096]{1,0:T(1,128)S(1)} fusion(f32[2048,1]{0,1:T(1,128)S(1)} %bitcast.476, f32[1,2048,4096]{2,1,0:T(8,128)} %param.1), kind=kOutput, calls=%fused_computation.14 | convolution fusion | flops 100663296 | bytes 33579008 | tf_op jit(solution)/shard_map/mij,mi->mj/dot_general | solution.py:43
  108.2 13.2 %all-gather.2 = f32[16384]{0:T(1024)S(1)} all-gather(f32[4096]{0:T(1024)S(1)} %bitcast.465), channel_id=4, replica_groups=mesh['grp'=4,'section'=2,'row'=4] {'row'}, dimensions={0}, use_global_device_ids=true | all-gather | bytes 81920 | tf_op jit(solution)/shard_map/all_gather | solution.py:44
  121.5 2.0 all-gather.3
  123.6 1.9 multiply_reduce_fusion.8
  127.1 0.6 multiply_reduce_fusion.20
  128.4 0.6 multiply_reduce_fusion.19
  129.0 0.7 convolution_bitcast_fusion.10
  129.7 0.7 convolution_bitcast_fusion.11
  131.1 19.5 %fusion.10 = f32[1,4096]{1,0:T(1,128)S(1)} fusion(f32[2048,1]{0,1:T(1,128)S(1)} %bitcast.474, f32[1,2048,4096]{2,1,0:T(8,128)} %param.1), kind=kOutput, calls=%fused_computation.12 | convolution fusion | flops 100663296 | bytes 33579008 | tf_op jit(solution)/shard_map/mij,mi->mj/dot_general | solution.py:43
  151.4 13.2 %all-gather.4 = f32[16384]{0:T(1024)S(1)} all-gather(f32[4096]{0:T(1024)S(1)} %bitcast.463), channel_id=6, replica_groups=mesh['grp'=4,'section'=2,'row'=4] {'row'}, dimensions={0}, use_global_device_ids=true | all-gather | bytes 81920 | tf_op jit(solution)/shard_map/all_gather | solution.py:44
  164.6 2.1 all-gather.5
  169.4 0.6 multiply_reduce_fusion.18
  170.8 0.6 multiply_reduce_fusion.17
  171.4 0.7 convolution_bitcast_fusion.8
  172.0 0.7 convolution_bitcast_fusion.9
  173.4 19.5 %fusion.8 = f32[1,4096]{1,0:T(1,128)S(1)} fusion(f32[2048,1]{0,1:T(1,128)S(1)} %bitcast.475, f32[1,2048,4096]{2,1,0:T(8,128)} %param.1), kind=kOutput, calls=%fused_computation.10 | convolution fusion | flops 100663296 | bytes 33579008 | tf_op jit(solution)/shard_map/mij,mi->mj/dot_general | solution.py:43
  193.8 13.2 %all-gather.6 = f32[16384]{0:T(1024)S(1)} all-gather(f32[4096]{0:T(1024)S(1)} %bitcast.464), channel_id=8, replica_groups=mesh['grp'=4,'section'=2,'row'=4] {'row'}, dimensions={0}, use_global_device_ids=true | all-gather | bytes 81920 | tf_op jit(solution)/shard_map/all_gather | solution.py:44
  207.1 2.3 all-gather.7
  209.4 0.6 multiply_reduce_fusion.6
  212.0 0.6 multiply_reduce_fusion.16
  213.3 0.6 multiply_reduce_fusion.15
  213.9 0.7 convolution_bitcast_fusion.6
  214.6 0.7 convolution_bitcast_fusion.7
  216.7 19.5 %fusion.6 = f32[1,4096]{1,0:T(1,128)S(1)} fusion(f32[2048,1]{0,1:T(1,128)S(1)} %bitcast.471, f32[1,2048,4096]{2,1,0:T(8,128)} %param.1), kind=kOutput, calls=%fused_computation.8 | convolution fusion | flops 100663296 | bytes 33579008 | tf_op jit(solution)/shard_map/mij,mi->mj/dot_general | solution.py:43
  236.2 13.1 %all-gather.8 = f32[16384]{0:T(1024)S(1)} all-gather(f32[4096]{0:T(1024)S(1)} %bitcast.466), channel_id=10, replica_groups=mesh['grp'=4,'section'=2,'row'=4] {'row'}, dimensions={0}, use_global_device_ids=true | all-gather | bytes 81920 | tf_op jit(solution)/shard_map/all_gather | solution.py:44
  249.4 2.0 all-gather.9
  251.4 0.6 multiply_reduce_fusion.5
  254.3 0.6 multiply_reduce_fusion.14
  255.6 0.6 multiply_reduce_fusion.13
  256.2 0.7 convolution_bitcast_fusion.4
  256.9 0.7 convolution_bitcast_fusion.5
  259.0 19.5 %fusion.4 = f32[1,4096]{1,0:T(1,128)S(1)} fusion(f32[2048,1]{0,1:T(1,128)S(1)} %bitcast.472, f32[1,2048,4096]{2,1,0:T(8,128)} %param.1), kind=kOutput, calls=%fused_computation.6 | convolution fusion | flops 100663296 | bytes 33579008 | tf_op jit(solution)/shard_map/mij,mi->mj/dot_general | solution.py:43
  278.5 13.2 %all-gather.10 = f32[16384]{0:T(1024)S(1)} all-gather(f32[4096]{0:T(1024)S(1)} %bitcast.467), channel_id=12, replica_groups=mesh['grp'=4,'section'=2,'row'=4] {'row'}, dimensions={0}, use_global_device_ids=true | all-gather | bytes 81920 | tf_op jit(solution)/shard_map/all_gather | solution.py:44
  291.7 2.0 all-gather.11
  293.8 0.6 multiply_reduce_fusion.4
  296.7 0.6 multiply_reduce_fusion.12
  298.0 0.6 multiply_reduce_fusion.11
  298.6 0.7 convolution_bitcast_fusion.2
  299.3 0.7 convolution_bitcast_fusion.3
  301.4 19.5 %fusion.2 = f32[1,4096]{1,0:T(1,128)S(1)} fusion(f32[2048,1]{0,1:T(1,128)S(1)} %bitcast.473, f32[1,2048,4096]{2,1,0:T(8,128)} %param.1), kind=kOutput, calls=%fused_computation.4 | convolution fusion | flops 100663296 | bytes 33579008 | tf_op jit(solution)/shard_map/mij,mi->mj/dot_general | solution.py:43
  320.9 13.2 %all-gather.12 = f32[16384]{0:T(1024)S(1)} all-gather(f32[4096]{0:T(1024)S(1)} %bitcast.468), channel_id=14, replica_groups=mesh['grp'=4,'section'=2,'row'=4] {'row'}, dimensions={0}, use_global_device_ids=true | all-gather | bytes 81920 | tf_op jit(solution)/shard_map/all_gather | solution.py:44
  334.2 2.1 all-gather.13
  339.3 0.6 multiply_reduce_fusion.10
  340.6 0.6 multiply_reduce_fusion.9
  341.2 0.7 convolution_bitcast_fusion
  341.9 0.7 convolution_bitcast_fusion.1
  344.0 19.5 %fusion = f32[1,4096]{1,0:T(1,128)S(1)} fusion(f32[2048,1]{0,1:T(1,128)S(1)} %bitcast.470, f32[1,2048,4096]{2,1,0:T(8,128)} %param.1), kind=kOutput, calls=%fused_computation.2 | convolution fusion | flops 100663296 | bytes 33579008 | tf_op jit(solution)/shard_map/mij,mi->mj/dot_general | solution.py:43
  363.9 13.2 %all-gather.14 = f32[16384]{0:T(1024)S(1)} all-gather(f32[4096]{0:T(1024)S(1)} %bitcast.462), channel_id=16, replica_groups=mesh['grp'=4,'section'=2,'row'=4] {'row'}, dimensions={0}, use_global_device_ids=true | all-gather | bytes 81920 | tf_op jit(solution)/shard_map/all_gather | solution.py:44
  377.1 2.1 all-gather.15
  380.9 30.3 %fusion.47 = f32[2048,4096]{1,0:T(8,128)} fusion(f32[1,8,8192]{2,1,0:T(8,128)S(1)} %stack.172, s32[]{:T(128)S(6)} %select_n.161, f32[1,8,8192]{2,1,0:T(8,128)S(1)} %stack.84, s32[]{:T(128)S(6)} %select_n.146), kind=kOutput, calls=%fused_computation.65 | convolution fusion | flops 805306368 | bytes 33751048 | tf_op jit(solution)/shard_map/mki,mkj->mij/dot_general | solution.py:62
  411.2 41.4 %bitcast_subtract_fusion = f32[1,2048,4096]{2,1,0:T(8,128)} fusion(f32[1,2048,4096]{2,1,0:T(8,128)} %param.1, f32[2048,4096]{1,0:T(8,128)} %fusion.47, f32[1,8,8192]{2,1,0:T(8,128)S(1)} %stack.84, s32[]{:T(128)S(6)} %select_n.161, f32[1,8,8192]{2,1,0:T(8,128)S(1)} %stack.172, s32[]{:T(128)S(6)} %select_n.146), kind=kOutput, calls=%fused_computation | convolution fusion | flops 822083584 | bytes 100859912 | tf_op jit(solution)/shard_map/mki,mkj->mij/dot_general | solution.py:63
  (88 shorter events, 17.5 us)
Async XLA Ops:
  6.5 23.6 %all-reduce.2.cloned.1.call-start = ((), (), s32[]{:S(2)}) async-start(), calls=%async_computation | async-start | bytes 131072 | tf_op jit(solution)/shard_map/psum | solution.py:12
Sparse Core Ops, SparseCore 0:
  9.6 20.4 all-reduce.1
